TPU v7x, 256 devices: a whole 4x4x8 slice. The times are simulated.
256 devices in a mesh: atom: 32 (over z, x_hi, core), kvec: 8 (over x_lo, y).
Axes of the slice: x: 4 (x_hi: 2, x_lo: 2; x = x_hi * 2 + x_lo), y: 4, z: 8, core: 2. Of those that a mesh axis runs over, the one named last changes fastest.
Arguments:
- scaled_coordinate_array: float32 [3, 524288], P(None, 'atom'), may hold values from 0 to 1
- particle_charge_list: float32 [524288], P('atom'), may hold values from -4 to 4
- reciprocal_triples: int32 [3, 4096], P(None, 'kvec'), may hold values from -128 to 128, as said below
Outputs:
- forces: float32 [3, 524288], P(None, 'atom')
- potential: float32 [524288], P('atom')
- energy: float32 [], replicated
Inputs may be any that keep to these rules, and one draw needn't show every extreme that they name: `reciprocal_triples`: every k-vector has a component of magnitude 64 or more.
All inputs are finite; a program needn't handle non-finite values.
Results may differ from a plain program's by a relative error of at most 0.0003.
Values sent between devices are 32-bit elements; how exact they have to be, the bound alone decides.
No kernel may reach another device: no remote copies, remote signals or barrier semaphores. Data moves between devices by JAX's collectives and lax.ppermute only.
A program may use at most 192 MiB of HBM per device.

v0:
```python
import functools
import math

import jax
import jax.numpy as jnp
from jax import lax
from jax.experimental import pallas as pl
from jax.experimental.pallas import tpu as pltpu
from jax.sharding import PartitionSpec as P

TOP = 128
STRIDE = 16
BLOCK = 4096
ROWS = BLOCK // 128
HALF = ROWS // 2
PART = 32
SLOTS = 8
WRITE_PART = 64
WRITE_SLOTS = 5
UNROLL = 16
GROUP = 8
TINY = 1e-6
KINDS = 5
MIB = 1 << 20


def rows_of(ref, start):
    return ref[pl.ds(pl.multiple_of(start, ROWS), ROWS), :]


def times(a, b):
    return a[0] * b[0] - a[1] * b[1], a[0] * b[1] + a[1] * b[0]


def turn(x):
    y = 4.0 * (x - jnp.round(x))
    n = jnp.round(y)
    r = (0.5 * math.pi) * (y - n)
    z = r * r
    s = r + r * z * (-1.6666654611e-1 + z * (8.3321608736e-3 - 1.9515295891e-4 * z))
    c = 4.166664568298827e-2 + z * (-1.388731625493765e-3 + 2.443315711809948e-5 * z)
    c = 1.0 + z * (c * z - 0.5)
    odd = jnp.abs(n) == 1.0
    cos = jnp.where(odd, s, c)
    sin = jnp.where(odd, c, s)
    cos = jnp.where((n > 0.5) | (n < -1.5), -cos, cos)
    sin = jnp.where((n > 1.5) | (n < -0.5), -sin, sin)
    return cos, sin


def fill_powers(x, weight, low, cos_ref, sin_ref, signed):
    small = [(jnp.ones_like(x), jnp.zeros_like(x)), turn(x)]
    for b in range(2, STRIDE // 2 + 1):
        small.append(times(small[b // 2], small[b - b // 2]))
    big = times(small[-1], small[-1])

    def put(h, c, s):
        def at(r):
            return pl.ds(pl.multiple_of(r * ROWS + low, 8), HALF)

        cos_ref[at(h)] = c
        if signed:
            sin_ref[at(TOP + h)] = s
            sin_ref[at(TOP - h)] = -s
        else:
            sin_ref[at(h)] = s

    def weighted(v):
        return v if weight is None else (weight * v[0], weight * v[1])

    for b in range(STRIDE // 2):
        put(b, *weighted(small[b]))

    def around(a, state, both):
        c, s = state
        put(STRIDE * a, c, s)
        for b in range(1, STRIDE // 2 + 1):
            cb, sb = small[b]
            cc, ss, sc, cs = c * cb, s * sb, s * cb, c * sb
            put(STRIDE * a - b, cc + ss, sc - cs)
            if both and b < STRIDE // 2:
                put(STRIDE * a + b, cc - ss, sc + cs)

    def step(a, state):
        around(a, state, True)
        return times(state, big)

    last = lax.fori_loop(1, TOP // STRIDE, step, weighted(big), unroll=TOP // STRIDE - 1)
    around(TOP // STRIDE, last, False)


def eighths(v):
    return (v[0:8] + v[8:16]) + (v[16:24] + v[24:32])


def nonzero(q):
    return jnp.where(jnp.abs(q) < TINY, TINY, q)


def lines(v):
    return [v[:, at : at + 128] for at in range(0, v.shape[1], 128)]


def to_scalars(stage, scalars, sems):
    return [
        pltpu.make_async_copy(stage.at[i], scalars.at[pl.ds(128 * i, 128)], sems.at[i])
        for i in range(stage.shape[0])
    ]


def half_space(triples):
    return jnp.where(triples[0:1] < 0, -triples, triples)


def phases_kernel(
    trip_hbm, x_hbm, q_hbm, e_ref, s_ref,
    xc, xs, yc, ys, zc, zs, acc_c, acc_s, trip_ref, x_ref, q_ref, in_sems,
    xyz, stage, idx, idx_sem, ring, sems,
):
    blocks, modes = e_ref.shape[0], e_ref.shape[1]
    parts = modes // WRITE_PART
    loads = [
        pltpu.make_async_copy(src, dst, in_sems.at[i])
        for i, (src, dst) in enumerate(((x_hbm, x_ref), (q_hbm, q_ref), (trip_hbm, trip_ref)))
    ]
    for load in loads:
        load.start()

    def clear(i, carry):
        at = pl.ds(pl.multiple_of(i * 128, 128), 128)
        acc_c[at] = jnp.zeros((128, 128), jnp.float32)
        acc_s[at] = jnp.zeros((128, 128), jnp.float32)
        return carry

    lax.fori_loop(0, acc_c.shape[0] // 128, clear, 0)
    for load in loads:
        load.wait()
    triples = half_space(trip_ref[...])
    h, k, l = triples[0:1], triples[1:2], triples[2:3]
    for kind, row in enumerate((h, jnp.abs(k), k + TOP, jnp.abs(l), l + TOP)):
        for r, line in enumerate(lines(ROWS * row)):
            at = kind * (modes // 128) + r
            stage[at : at + 1] = line
    for move in to_scalars(stage, idx, idx_sem):
        move.start()

    def fold(i, carry):
        for d in range(3):
            xyz[d, pl.ds(i, 1)] = x_ref[d : d + 1, pl.ds(pl.multiple_of(i * 128, 128), 128)]
        return carry

    lax.fori_loop(0, xyz.shape[1], fold, 0, unroll=16)
    faint = jnp.max(jnp.where(jnp.abs(q_ref[...]) < TINY, 1.0, 0.0)) > 0.0

    def copy(slot, b, p):
        return pltpu.make_async_copy(
            ring.at[slot], e_ref.at[b, pl.ds(p * WRITE_PART, WRITE_PART)], sems.at[slot]
        )

    def block(b, carry):
        for low in (0, HALF):
            here = pl.ds(pl.multiple_of(b * ROWS + low, HALF), HALF)
            for d, (c_ref, s_ref_) in enumerate(((xc, xs), (yc, ys), (zc, zs))):
                weight = nonzero(q_ref[here]) if d == 2 else None
                fill_powers(xyz[d, here], weight, low, c_ref, s_ref_, d > 0)

        @pl.when(b == 0)
        def _():
            for move in to_scalars(stage, idx, idx_sem):
                move.wait()

        def part(p, carry):
            t = b * parts + p
            slot = lax.rem(t, WRITE_SLOTS)

            @pl.when(t >= WRITE_SLOTS)
            def _():
                copy(slot, b, p).wait()

            def group(g, ratio):
                sums_c, sums_s = [], []
                for j in range(GROUP):
                    i = g * GROUP + j
                    k = p * WRITE_PART + i
                    h = idx[k]
                    first = rows_of(xc, h), rows_of(xs, h)
                    second = rows_of(yc, idx[modes + k]), rows_of(ys, idx[2 * modes + k])
                    third = rows_of(zc, idx[3 * modes + k]), rows_of(zs, idx[4 * modes + k])
                    c, s = times(times(first, second), third)
                    ring[slot, i, 0] = c
                    ring[slot, i, 1] = s
                    if ratio is not None:
                        c, s = ratio * c, ratio * s
                    sums_c.append(eighths(c))
                    sums_s.append(eighths(s))
                at = pl.ds(pl.multiple_of((p * WRITE_PART + g * GROUP) * 8, 8 * GROUP), 8 * GROUP)
                sums_c = acc_c[at] + jnp.concatenate(sums_c, axis=0)
                sums_s = acc_s[at] + jnp.concatenate(sums_s, axis=0)
                acc_c[at] = sums_c
                acc_s[at] = sums_s

            groups = WRITE_PART // GROUP

            @pl.when(faint)
            def _():
                q = q_ref[pl.ds(pl.multiple_of(b * ROWS, ROWS), ROWS)]
                ratio = q / nonzero(q)
                lax.fori_loop(0, groups, lambda g, c: (group(g, ratio), c)[1], 0)

            @pl.when(jnp.logical_not(faint))
            def _():
                lax.fori_loop(0, groups, lambda g, c: (group(g, None), c)[1], 0, unroll=UNROLL // GROUP)

            copy(slot, b, p).start()
            return carry

        return lax.fori_loop(0, parts, part, carry)

    lax.fori_loop(0, blocks, block, 0)

    for half, acc in enumerate((acc_c, acc_s)):
        for r in range(modes // 128):
            rows = acc[pl.ds(1024 * r, 128, stride=8)]
            for sub in range(1, 8):
                rows = rows + acc[pl.ds(1024 * r + sub, 128, stride=8)]
            at = half * (modes // 128) + r
            s_ref[at : at + 1] = jnp.sum(rows.T, axis=0, keepdims=True)

    def drain(slot, carry):
        copy(slot, 0, 0).wait()
        return carry

    lax.fori_loop(0, WRITE_SLOTS, drain, 0)


def response_kernel(scale, got_ref, trip_ref, e_ref, o_ref, stage, w, w_sem, ring, sems):
    blocks, modes = e_ref.shape[0], e_ref.shape[1]
    parts = modes // PART
    n_lines = modes // 128

    def copy(slot, b, p):
        return pltpu.make_async_copy(
            e_ref.at[b, pl.ds(p * PART, PART)], ring.at[slot], sems.at[slot]
        )

    def fetch(t):
        copy(lax.rem(t, SLOTS), t // parts, lax.rem(t, parts)).start()

    def first(t, carry):
        fetch(t)
        return carry

    lax.fori_loop(0, SLOTS, first, 0)

    total = got_ref[0]
    for i in range(1, got_ref.shape[0]):
        total = total + got_ref[i]
    cosine, sine = total[:n_lines], total[n_lines:]
    triples = half_space(trip_ref[...])
    table = [
        (2.0 * math.pi) * jnp.concatenate(lines(triples[d : d + 1]), axis=0).astype(jnp.float32)
        for d in range(3)
    ]
    norm = table[0] * table[0] + table[1] * table[1] + table[2] * table[2]
    damping = 4.0 * math.pi * jnp.exp(-norm / 1600000.0) / norm
    energy = scale * jnp.sum(damping * (cosine * cosine + sine * sine))
    for kind, rows in enumerate([damping * cosine, damping * sine] + table):
        stage[kind * n_lines : (kind + 1) * n_lines] = rows
    for move in to_scalars(stage, w, w_sem):
        move.start()
    for move in to_scalars(stage, w, w_sem):
        move.wait()
    zero = jnp.zeros((ROWS, 128), jnp.float32)

    def block(b, carry):
        def part(p, state):
            t = b * parts + p
            slot = lax.rem(t, SLOTS)
            copy(slot, b, p).wait()

            def mode(i, state):
                f0, f1, f2, pot = state
                k = p * PART + i
                wr, wi = w[k], w[modes + k]
                c = ring[slot, i, 0]
                s = ring[slot, i, 1]
                pot = pot + (wr * c + wi * s)
                g = wr * s - wi * c
                return (
                    f0 + w[2 * modes + k] * g,
                    f1 + w[3 * modes + k] * g,
                    f2 + w[4 * modes + k] * g,
                    pot,
                )

            state = lax.fori_loop(0, PART, mode, state, unroll=UNROLL)

            @pl.when(t + SLOTS < blocks * parts)
            def _():
                fetch(t + SLOTS)

            return state

        state = lax.fori_loop(0, parts, part, (zero,) * 4)
        for t in range(2):
            for c in range(4):
                o_ref[2 * b + t, HALF * c : HALF * (c + 1)] = state[c][HALF * t : HALF * (t + 1)]
            o_ref[2 * b + t, 4 * HALF :] = jnp.full((8, 128), energy, jnp.float32)
        return carry

    lax.fori_loop(0, blocks, block, 0)


def on_device(scaled_coordinate_array, particle_charge_list, reciprocal_triples):
    local_atoms = scaled_coordinate_array.shape[1]
    modes = reciprocal_triples.shape[1]
    n_atom = lax.axis_size("atom")
    n_kvec = lax.axis_size("kvec")
    natoms = local_atoms * n_atom
    blocks = local_atoms // BLOCK
    n_lines = modes // 128
    q = particle_charge_list.reshape(local_atoms // 128, 128)

    vmem = pl.BlockSpec(memory_space=pltpu.VMEM)
    hbm = pl.BlockSpec(memory_space=pl.ANY)
    def ring(slots, part):
        return [
            pltpu.VMEM((slots, part, 2, ROWS, 128), jnp.float32),
            pltpu.SemaphoreType.DMA((slots,)),
        ]

    def scalars(dtype):
        return [
            pltpu.VMEM((KINDS * n_lines, 128), dtype),
            pltpu.SMEM((KINDS * modes,), dtype),
            pltpu.SemaphoreType.DMA((KINDS * n_lines,)),
        ]

    positive = pltpu.VMEM(((TOP + 1) * ROWS, 128), jnp.float32)
    both = pltpu.VMEM(((2 * TOP + 1) * ROWS, 128), jnp.float32)
    e, share = pl.pallas_call(
        phases_kernel,
        in_specs=[hbm, hbm, hbm],
        out_specs=[hbm, vmem],
        out_shape=[
            jax.ShapeDtypeStruct((blocks, modes, 2, ROWS, 128), jnp.float32),
            jax.ShapeDtypeStruct((8, 128), jnp.float32),
        ],
        scratch_shapes=[
            positive,
            positive,
            positive,
            both,
            positive,
            both,
            pltpu.VMEM((modes * 8, 128), jnp.float32),
            pltpu.VMEM((modes * 8, 128), jnp.float32),
            pltpu.VMEM((3, modes), jnp.int32),
            pltpu.VMEM((3, local_atoms), jnp.float32),
            pltpu.VMEM((local_atoms // 128, 128), jnp.float32),
            pltpu.SemaphoreType.DMA((3,)),
            pltpu.VMEM((3, local_atoms // 128, 128), jnp.float32),
        ]
        + scalars(jnp.int32)
        + ring(WRITE_SLOTS, WRITE_PART),
        compiler_params=pltpu.CompilerParams(vmem_limit_bytes=48 * MIB),
    )(reciprocal_triples, scaled_coordinate_array, q)

    share = share + lax.ppermute(share, "atom", [(i, i ^ 1) for i in range(n_atom)])
    share = jnp.broadcast_to(share[None], (n_atom // 2, 8, 128))
    cores = [[c + 2 * m for m in range(n_atom // 2)] for c in range(2)]
    got = lax.all_to_all(share, "atom", 0, 0, tiled=True, axis_index_groups=cores)

    terms = pl.pallas_call(
        functools.partial(response_kernel, 50.0 / natoms),
        in_specs=[vmem, vmem, hbm],
        out_specs=vmem,
        out_shape=jax.ShapeDtypeStruct((n_kvec, 4 * HALF + 8, 128), jnp.float32),
        scratch_shapes=scalars(jnp.float32) + ring(SLOTS, PART),
        compiler_params=pltpu.CompilerParams(vmem_limit_bytes=24 * MIB),
    )(got, reciprocal_triples, e)

    own = lax.all_to_all(terms, "kvec", 0, 0, tiled=True).sum(axis=0)
    energy = own[4 * HALF, 0]
    copies = jnp.broadcast_to(own[None, : 4 * HALF], (n_kvec, 4 * HALF, 128))
    summed = lax.all_to_all(copies, "kvec", 0, 0, tiled=True)
    summed = summed.reshape(n_kvec, 4, HALF * 128).transpose(1, 0, 2).reshape(4, local_atoms)
    scale = 1.0 / math.sqrt(natoms)
    forces = summed[:3] * scale
    potential = summed[3] * (400.0 * scale) / nonzero(particle_charge_list)
    return (forces, potential, energy)


def solution(mesh):
    return jax.shard_map(
        on_device,
        mesh=mesh,
        in_specs=(P(None, "atom"), P("atom"), P(None, "kvec")),
        out_specs=(P(None, "atom"), P("atom"), P()),
        check_vma=False,
    )
```

profile of v0, /device:TPU:2, one launch (start us, length us, event | category | flops | bytes accessed | tf_op | source)
XLA Modules:
  0.0 97.2 jit_solution(14312153678904372241)
XLA Ops:
  0.6 0.0 copy-start
  0.6 0.9 copy-done
  1.6 0.0 copy-start.1
  1.6 0.8 copy-done.1
  2.4 0.0 copy-start.3
  2.4 0.7 copy-done.3
  3.1 0.0 copy-start.2
  3.1 26.5 %shard_map.58 = (f32[4,512,2,32,128]{4,3,2,1,0:T(8,128)}, f32[8,128]{1,0:T(8,128)S(1)}) custom-call(s32[3,512]{1,0:T(4,128)S(1)} %copy-done.3, f32[3,16384]{1,0:T(4,128)S(1)} %copy-done, f32[128,128]{1,0:T(8,128)S(1)} %bitcast.5), custom_call_target="tpu_custom_call" | custom-call | tf_op jit(solution)/shard_map/pallas_call | solution.py:341
  29.6 0.1 collective-permute-start
  29.7 1.2 %collective-permute-done = f32[8,128]{1,0:T(8,128)S(1)} collective-permute-done((f32[8,128]{1,0:T(8,128)S(1)}, f32[8,128]{1,0:T(8,128)S(1)}, u32[]{:S(2)}, u32[]{:S(2)}) %collective-permute-start) | collective-permute-done | bytes 4128 | tf_op jit(solution)/shard_map/ppermute | solution.py:369
  30.9 20.5 %all_to_all.15.got_ref = f32[16,8,128]{2,1,0:T(8,128)S(1)} all-to-all(f32[16,8,128]{2,1,0:T(8,128)S(1)} %broadcast_in_dim.5), channel_id=1, replica_groups={{0,16,32,48,64,80,96,112,128,144,160,176,192,208,224,240},{8,24,40,56,7..., dimensions={0} | all-to-all | bytes 131072 | tf_op jit(solution)/shard_map/all_to_all | solution.py:372
  51.3 20.9 %shard_map.59 = f32[8,72,128]{2,1,0:T(8,128)S(1)} custom-call(f32[16,8,128]{2,1,0:T(8,128)S(1)} %all_to_all.15.got_ref, s32[3,512]{1,0:T(4,128)S(1)} %copy-done.3, f32[4,512,2,32,128]{4,3,2,1,0:T(8,128)} %get-tuple-element.6.e_ref), custom_call_target="tpu_custom_call" | custom-call | tf_op jit(solution)/shard_map/pallas_call | solution.py:374
  72.2 11.9 %all_to_all.16 = f32[8,72,128]{2,1,0:T(8,128)S(1)} all-to-all(f32[8,72,128]{2,1,0:T(8,128)S(1)} %shard_map.59), channel_id=1, replica_groups=mesh['atom'=32,'kvec'=8] {'kvec'}, dimensions={0} | all-to-all | bytes 589824 | tf_op jit(solution)/shard_map/all_to_all | solution.py:383
  84.2 0.7 broadcast_in_dim.6
  84.9 4.8 %all-to-all-start.2 = ((f32[8,64,128]{2,1,0:T(8,128)}), f32[8,64,128]{2,1,0:T(8,128)S(1)}, u32[]{:S(2)}, u32[]{:S(2)}) async-start(f32[8,64,128]{2,1,0:T(8,128)} %broadcast_in_dim.6), calls=%async_computation.2 | async-start | bytes 524288 | tf_op jit(solution)/shard_map/all_to_all | solution.py:386
  89.7 0.5 slice.21
  90.2 5.3 %all-to-all-done.2 = f32[8,64,128]{2,1,0:T(8,128)S(1)} async-done(((f32[8,64,128]{2,1,0:T(8,128)}), f32[8,64,128]{2,1,0:T(8,128)S(1)}, u32[]{:S(2)}, u32[]{:S(2)}) %all-to-all-start.2) | async-done | bytes 262176 | tf_op jit(solution)/shard_map/all_to_all | solution.py:386
  95.6 0.1 reshape.23
  95.7 0.1 slice_multiply_fusion.1
  95.8 0.8 slice_multiply_fusion
  96.5 0.0 copy-done.2
  96.6 0.6 select_divide_fusion
  (4 shorter events, 0.0 us)
Async XLA Ops:
  0.6 1.0 copy-start
  1.6 0.8 copy-start.1
  2.4 0.7 copy-start.3
  3.1 93.4 %copy-start.2 = (f32[16384]{0:T(1024)S(1)}, f32[16384]{0:T(1024)}, u32[]{:S(2)}) copy-start(f32[16384]{0:T(1024)} %param.4) | copy-start | bytes 196612
  29.6 1.3 %collective-permute-start = (f32[8,128]{1,0:T(8,128)S(1)}, f32[8,128]{1,0:T(8,128)S(1)}, u32[]{:S(2)}, u32[]{:S(2)}) collective-permute-start(f32[8,128]{1,0:T(8,128)S(1)} %get-tuple-element.5), channel_id=1, source_target_pairs={{0,8},{8,0},{16,24},{24,16},{32,40},{40,32},{48,56},{56,48},{64,72... | collective-permute-start | bytes 12296 | tf_op jit(solution)/shard_map/ppermute | solution.py:369
  84.9 10.6 %all-to-all-start.2 = ((f32[8,64,128]{2,1,0:T(8,128)}), f32[8,64,128]{2,1,0:T(8,128)S(1)}, u32[]{:S(2)}, u32[]{:S(2)}) async-start(f32[8,64,128]{2,1,0:T(8,128)} %broadcast_in_dim.6), calls=%async_computation.2 | async-start | bytes 524288 | tf_op jit(solution)/shard_map/all_to_all | solution.py:386
where the time goes:
time: 97.6 us; the launch traced here: 97.2 us
  Pallas kernels  47.4 us (49%)
  blocking collectives  32.4 us (33%)
  waiting for transfers between devices  6.49 us (7%)
  starting transfers between devices  4.89 us (5%)
  local copies, waits for them, and re-layouts  3.82 us (4%)
  other arithmetic  1.54 us (2%)
    pallas_call x1, Pallas kernels, on_device(): pl.pallas_call(phases_kernel, in_specs=[hbm, hbm, hbm], out_specs=[hbm, v...  26.5 us
    pallas_call x1, Pallas kernels, on_device(): pl.pallas_call(functools.partial(response_kernel, 50.0 / natoms), in_spec...  20.9 us
    all_to_all x1, blocking collectives, on_device(): lax.all_to_all(share, 'atom', 0, 0, tiled=True, axis_index_groups=cores)  20.5 us
    all_to_all x1, blocking collectives, on_device(): own = lax.all_to_all(terms, 'kvec', 0, 0, tiled=True).sum(axis=0)  11.9 us
    all_to_all x1, waiting for transfers between devices, on_device(): summed = lax.all_to_all(copies, 'kvec', 0, 0, tiled=True)  5.33 us
    all_to_all x1, starting transfers between devices, on_device(): summed = lax.all_to_all(copies, 'kvec', 0, 0, tiled=True)  4.8 us
    unnamed x8, local copies, waits for them, and re-layouts  2.48 us
  transfers between devices with their start and end apart: 2, of which 2 were waited for; matrix products, arithmetic and copies ran while one was open for 1% of the time, Pallas kernels for 0%

commit v1 on v0

--- a/solution.py
+++ b/solution.py
@@ -14,7 +14,7 @@
 ROWS = BLOCK // 128
 HALF = ROWS // 2
 PART = 32
-SLOTS = 8
+SLOTS = 12
 WRITE_PART = 64
 WRITE_SLOTS = 5
 UNROLL = 16
@@ -322,7 +322,7 @@
     q = particle_charge_list.reshape(local_atoms // 128, 128)
 
     vmem = pl.BlockSpec(memory_space=pltpu.VMEM)
-    hbm = pl.BlockSpec(memory_space=pl.ANY)
+    hbm = pl.BlockSpec(memory_space=pltpu.HBM)
     def ring(slots, part):
         return [
             pltpu.VMEM((slots, part, 2, ROWS, 128), jnp.float32),
@@ -344,7 +344,7 @@
         out_specs=[hbm, vmem],
         out_shape=[
             jax.ShapeDtypeStruct((blocks, modes, 2, ROWS, 128), jnp.float32),
-            jax.ShapeDtypeStruct((8, 128), jnp.float32),
+            pltpu.VMEM((8, 128), jnp.float32),
         ],
         scratch_shapes=[
             positive,
@@ -363,7 +363,7 @@
         ]
         + scalars(jnp.int32)
         + ring(WRITE_SLOTS, WRITE_PART),
-        compiler_params=pltpu.CompilerParams(vmem_limit_bytes=48 * MIB),
+        compiler_params=pltpu.CompilerParams(vmem_limit_bytes=58 * MIB),
     )(reciprocal_triples, scaled_coordinate_array, q)
 
     share = share + lax.ppermute(share, "atom", [(i, i ^ 1) for i in range(n_atom)])
@@ -377,7 +377,7 @@
         out_specs=vmem,
         out_shape=jax.ShapeDtypeStruct((n_kvec, 4 * HALF + 8, 128), jnp.float32),
         scratch_shapes=scalars(jnp.float32) + ring(SLOTS, PART),
-        compiler_params=pltpu.CompilerParams(vmem_limit_bytes=24 * MIB),
+        compiler_params=pltpu.CompilerParams(vmem_limit_bytes=32 * MIB),
     )(got, reciprocal_triples, e)
 
     own = lax.all_to_all(terms, "kvec", 0, 0, tiled=True).sum(axis=0)

time: 97.6 us -> 96.4 us (0.988)
  local copies, waits for them, and re-layouts: 3.82 us -> 2.04 us
    unnamed x8 -> x4, local copies, waits for them, and re-layouts: 2.48 us -> 0.7 us
where the time goes in v1:
time: 96.4 us; the launch traced here: 96 us
  Pallas kernels  48 us (50%)
  blocking collectives  32.4 us (34%)
  waiting for transfers between devices  6.49 us (7%)
  starting transfers between devices  4.89 us (5%)
  local copies, waits for them, and re-layouts  2.04 us (2%)
  other arithmetic  1.54 us (2%)
    pallas_call x1, Pallas kernels, on_device(): pl.pallas_call(phases_kernel, in_specs=[hbm, hbm, hbm], out_specs=[hbm, v...  27 us
    pallas_call x1, Pallas kernels, on_device(): pl.pallas_call(functools.partial(response_kernel, 50.0 / natoms), in_spec...  20.9 us
    all_to_all x1, blocking collectives, on_device(): lax.all_to_all(share, 'atom', 0, 0, tiled=True, axis_index_groups=cores)  20.5 us
    all_to_all x1, blocking collectives, on_device(): own = lax.all_to_all(terms, 'kvec', 0, 0, tiled=True).sum(axis=0)  11.9 us
    all_to_all x1, waiting for transfers between devices, on_device(): summed = lax.all_to_all(copies, 'kvec', 0, 0, tiled=True)  5.33 us
    all_to_all x1, starting transfers between devices, on_device(): summed = lax.all_to_all(copies, 'kvec', 0, 0, tiled=True)  4.8 us
  transfers between devices with their start and end apart: 2, of which 2 were waited for; matrix products, arithmetic and copies ran while one was open for 1% of the time, Pallas kernels for 0%

profile of v1, /device:TPU:2, one launch (start us, length us, event | category | flops | bytes accessed | tf_op | source)
XLA Modules:
  0.0 96.0 jit_solution(2109862030995554425)
XLA Ops:
  0.6 0.0 copy-start.1
  0.6 27.0 %shard_map.58 = (f32[4,512,2,32,128]{4,3,2,1,0:T(8,128)}, f32[8,128]{1,0:T(8,128)S(1)}) custom-call(s32[3,512]{1,0:T(4,128)} %trip_ref.1, f32[3,16384]{1,0:T(4,128)} %x_hbm.1, f32[128,128]{1,0:T(8,128)} %bitcast.9), custom_call_target="tpu_custom_call" | custom-call | tf_op jit(solution)/shard_map/pallas_call | solution.py:341
  27.7 0.1 collective-permute-start
  27.8 1.2 %collective-permute-done = f32[8,128]{1,0:T(8,128)S(1)} collective-permute-done((f32[8,128]{1,0:T(8,128)S(1)}, f32[8,128]{1,0:T(8,128)S(1)}, u32[]{:S(2)}, u32[]{:S(2)}) %collective-permute-start) | collective-permute-done | bytes 4128 | tf_op jit(solution)/shard_map/ppermute | solution.py:369
  28.9 20.5 %all_to_all.15.got_ref = f32[16,8,128]{2,1,0:T(8,128)S(1)} all-to-all(f32[16,8,128]{2,1,0:T(8,128)S(1)} %broadcast_in_dim.5), channel_id=1, replica_groups={{0,16,32,48,64,80,96,112,128,144,160,176,192,208,224,240},{8,24,40,56,7..., dimensions={0} | all-to-all | bytes 131072 | tf_op jit(solution)/shard_map/all_to_all | solution.py:372
  49.4 0.0 copy-start
  49.4 0.7 copy-done
  50.1 20.9 %shard_map.59 = f32[8,72,128]{2,1,0:T(8,128)S(1)} custom-call(f32[16,8,128]{2,1,0:T(8,128)S(1)} %all_to_all.15.got_ref, s32[3,512]{1,0:T(4,128)S(1)} %copy-done, f32[4,512,2,32,128]{4,3,2,1,0:T(8,128)} %get-tuple-element.6.e_ref), custom_call_target="tpu_custom_call" | custom-call | tf_op jit(solution)/shard_map/pallas_call | solution.py:374
  71.1 11.9 %all_to_all.16 = f32[8,72,128]{2,1,0:T(8,128)S(1)} all-to-all(f32[8,72,128]{2,1,0:T(8,128)S(1)} %shard_map.59), channel_id=1, replica_groups=mesh['atom'=32,'kvec'=8] {'kvec'}, dimensions={0} | all-to-all | bytes 589824 | tf_op jit(solution)/shard_map/all_to_all | solution.py:383
  83.0 0.7 broadcast_in_dim.6
  83.8 4.8 %all-to-all-start.2 = ((f32[8,64,128]{2,1,0:T(8,128)}), f32[8,64,128]{2,1,0:T(8,128)S(1)}, u32[]{:S(2)}, u32[]{:S(2)}) async-start(f32[8,64,128]{2,1,0:T(8,128)} %broadcast_in_dim.6), calls=%async_computation.2 | async-start | bytes 524288 | tf_op jit(solution)/shard_map/all_to_all | solution.py:386
  88.6 0.5 slice.21
  89.1 5.3 %all-to-all-done.2 = f32[8,64,128]{2,1,0:T(8,128)S(1)} async-done(((f32[8,64,128]{2,1,0:T(8,128)}), f32[8,64,128]{2,1,0:T(8,128)S(1)}, u32[]{:S(2)}, u32[]{:S(2)}) %all-to-all-start.2) | async-done | bytes 262176 | tf_op jit(solution)/shard_map/all_to_all | solution.py:386
  94.4 0.1 reshape.23
  94.5 0.1 slice_multiply_fusion.1
  94.6 0.8 slice_multiply_fusion
  95.4 0.0 copy-done.1
  95.4 0.6 select_divide_fusion
  (4 shorter events, 0.0 us)
Async XLA Ops:
  0.6 94.8 %copy-start.1 = (f32[16384]{0:T(1024)S(1)}, f32[16384]{0:T(1024)}, u32[]{:S(2)}) copy-start(f32[16384]{0:T(1024)} %param.4) | copy-start | bytes 196612
  27.7 1.3 %collective-permute-start = (f32[8,128]{1,0:T(8,128)S(1)}, f32[8,128]{1,0:T(8,128)S(1)}, u32[]{:S(2)}, u32[]{:S(2)}) collective-permute-start(f32[8,128]{1,0:T(8,128)S(1)} %get-tuple-element.5), channel_id=1, source_target_pairs={{0,8},{8,0},{16,24},{24,16},{32,40},{40,32},{48,56},{56,48},{64,72... | collective-permute-start | bytes 12296 | tf_op jit(solution)/shard_map/ppermute | solution.py:369
  49.4 0.7 copy-start
  83.8 10.6 %all-to-all-start.2 = ((f32[8,64,128]{2,1,0:T(8,128)}), f32[8,64,128]{2,1,0:T(8,128)S(1)}, u32[]{:S(2)}, u32[]{:S(2)}) async-start(f32[8,64,128]{2,1,0:T(8,128)} %broadcast_in_dim.6), calls=%async_computation.2 | async-start | bytes 524288 | tf_op jit(solution)/shard_map/all_to_all | solution.py:386

commit v2 on v1

--- a/solution.py
+++ b/solution.py
@@ -17,6 +17,7 @@
 SLOTS = 12
 WRITE_PART = 64
 WRITE_SLOTS = 5
+KEEP = 64
 UNROLL = 16
 GROUP = 8
 TINY = 1e-6
@@ -113,7 +114,7 @@
 
 
 def phases_kernel(
-    trip_hbm, x_hbm, q_hbm, e_ref, s_ref,
+    trip_hbm, x_hbm, q_hbm, e_ref, s_ref, keep_ref, modes_ref,
     xc, xs, yc, ys, zc, zs, acc_c, acc_s, trip_ref, x_ref, q_ref, in_sems,
     xyz, stage, idx, idx_sem, ring, sems,
 ):
@@ -143,6 +144,15 @@
             stage[at : at + 1] = line
     for move in to_scalars(stage, idx, idx_sem):
         move.start()
+    n_lines = modes // 128
+    table = [
+        (2.0 * math.pi) * jnp.concatenate(lines(triples[d : d + 1]), axis=0).astype(jnp.float32)
+        for d in range(3)
+    ]
+    norm = table[0] * table[0] + table[1] * table[1] + table[2] * table[2]
+    modes_ref[:n_lines] = 4.0 * math.pi * jnp.exp(-norm / 1600000.0) / norm
+    for d in range(3):
+        modes_ref[n_lines * (d + 1) : n_lines * (d + 2)] = table[d]
 
     def fold(i, carry):
         for d in range(3):
@@ -177,46 +187,52 @@
             def _():
                 copy(slot, b, p).wait()
 
-            def group(g, ratio):
-                sums_c, sums_s = [], []
-                for j in range(GROUP):
-                    i = g * GROUP + j
-                    k = p * WRITE_PART + i
-                    h = idx[k]
-                    first = rows_of(xc, h), rows_of(xs, h)
-                    second = rows_of(yc, idx[modes + k]), rows_of(ys, idx[2 * modes + k])
-                    third = rows_of(zc, idx[3 * modes + k]), rows_of(zs, idx[4 * modes + k])
-                    c, s = times(times(first, second), third)
-                    ring[slot, i, 0] = c
-                    ring[slot, i, 1] = s
-                    if ratio is not None:
-                        c, s = ratio * c, ratio * s
-                    sums_c.append(eighths(c))
-                    sums_s.append(eighths(s))
-                at = pl.ds(pl.multiple_of((p * WRITE_PART + g * GROUP) * 8, 8 * GROUP), 8 * GROUP)
-                sums_c = acc_c[at] + jnp.concatenate(sums_c, axis=0)
-                sums_s = acc_s[at] + jnp.concatenate(sums_s, axis=0)
-                acc_c[at] = sums_c
-                acc_s[at] = sums_s
-
-            groups = WRITE_PART // GROUP
-
-            @pl.when(faint)
-            def _():
-                q = q_ref[pl.ds(pl.multiple_of(b * ROWS, ROWS), ROWS)]
-                ratio = q / nonzero(q)
-                lax.fori_loop(0, groups, lambda g, c: (group(g, ratio), c)[1], 0)
-
-            @pl.when(jnp.logical_not(faint))
-            def _():
-                lax.fori_loop(0, groups, lambda g, c: (group(g, None), c)[1], 0, unroll=UNROLL // GROUP)
-
+            run(ring.at[slot], b, p * WRITE_PART)
             copy(slot, b, p).start()
             return carry
 
-        return lax.fori_loop(0, parts, part, carry)
+        kept = jnp.where(b == blocks - 1, KEEP // WRITE_PART, 0)
+        return lax.fori_loop(0, parts - kept, part, carry)
+
+    def run(out, b, start):
+        def group(g, ratio):
+            sums_c, sums_s = [], []
+            for j in range(GROUP):
+                i = g * GROUP + j
+                k = start + i
+                h = idx[k]
+                first = rows_of(xc, h), rows_of(xs, h)
+                second = rows_of(yc, idx[modes + k]), rows_of(ys, idx[2 * modes + k])
+                third = rows_of(zc, idx[3 * modes + k]), rows_of(zs, idx[4 * modes + k])
+                c, s = times(times(first, second), third)
+                out[i, 0] = c
+                out[i, 1] = s
+                if ratio is not None:
+                    c, s = ratio * c, ratio * s
+                sums_c.append(eighths(c))
+                sums_s.append(eighths(s))
+            at = pl.ds(pl.multiple_of((start + g * GROUP) * 8, 8 * GROUP), 8 * GROUP)
+            sums_c = acc_c[at] + jnp.concatenate(sums_c, axis=0)
+            sums_s = acc_s[at] + jnp.concatenate(sums_s, axis=0)
+            acc_c[at] = sums_c
+            acc_s[at] = sums_s
+
+        groups = out.shape[0] // GROUP
+
+        @pl.when(faint)
+        def _():
+            q = q_ref[pl.ds(pl.multiple_of(b * ROWS, ROWS), ROWS)]
+            ratio = q / nonzero(q)
+            lax.fori_loop(0, groups, lambda g, c: (group(g, ratio), c)[1], 0)
+
+        @pl.when(jnp.logical_not(faint))
+        def _():
+            lax.fori_loop(
+                0, groups, lambda g, c: (group(g, None), c)[1], 0, unroll=UNROLL // GROUP
+            )
 
     lax.fori_loop(0, blocks, block, 0)
+    run(keep_ref, blocks - 1, modes - KEEP)
 
     for half, acc in enumerate((acc_c, acc_s)):
         for r in range(modes // 128):
@@ -233,10 +249,12 @@
     lax.fori_loop(0, WRITE_SLOTS, drain, 0)
 
 
-def response_kernel(scale, got_ref, trip_ref, e_ref, o_ref, stage, w, w_sem, ring, sems):
+def response_kernel(scale, got_ref, modes_ref, keep_ref, e_ref, o_ref, stage, w, w_sem, ring, sems):
     blocks, modes = e_ref.shape[0], e_ref.shape[1]
     parts = modes // PART
     n_lines = modes // 128
+    lead = (modes - KEEP) // PART
+    n_parts = blocks * parts - KEEP // PART
 
     def copy(slot, b, p):
         return pltpu.make_async_copy(
@@ -244,7 +262,9 @@
         )
 
     def fetch(t):
-        copy(lax.rem(t, SLOTS), t // parts, lax.rem(t, parts)).start()
+        later = t - lead
+        b = jnp.where(later < 0, blocks - 1, later // parts)
+        copy(lax.rem(t, SLOTS), b, jnp.where(later < 0, t, lax.rem(later, parts))).start()
 
     def first(t, carry):
         fetch(t)
@@ -256,59 +276,61 @@
     for i in range(1, got_ref.shape[0]):
         total = total + got_ref[i]
     cosine, sine = total[:n_lines], total[n_lines:]
-    triples = half_space(trip_ref[...])
-    table = [
-        (2.0 * math.pi) * jnp.concatenate(lines(triples[d : d + 1]), axis=0).astype(jnp.float32)
-        for d in range(3)
-    ]
-    norm = table[0] * table[0] + table[1] * table[1] + table[2] * table[2]
-    damping = 4.0 * math.pi * jnp.exp(-norm / 1600000.0) / norm
+    damping = modes_ref[:n_lines]
     energy = scale * jnp.sum(damping * (cosine * cosine + sine * sine))
-    for kind, rows in enumerate([damping * cosine, damping * sine] + table):
-        stage[kind * n_lines : (kind + 1) * n_lines] = rows
+    stage[:n_lines] = damping * cosine
+    stage[n_lines : 2 * n_lines] = damping * sine
+    stage[2 * n_lines :] = modes_ref[n_lines:]
     for move in to_scalars(stage, w, w_sem):
         move.start()
     for move in to_scalars(stage, w, w_sem):
         move.wait()
     zero = jnp.zeros((ROWS, 128), jnp.float32)
 
-    def block(b, carry):
+    def run(source, start, state):
+        def mode(i, state):
+            f0, f1, f2, pot = state
+            k = start + i
+            wr, wi = w[k], w[modes + k]
+            c = source[i, 0]
+            s = source[i, 1]
+            pot = pot + (wr * c + wi * s)
+            g = wr * s - wi * c
+            return (
+                f0 + w[2 * modes + k] * g,
+                f1 + w[3 * modes + k] * g,
+                f2 + w[4 * modes + k] * g,
+                pot,
+            )
+
+        return lax.fori_loop(0, source.shape[0], mode, state, unroll=UNROLL)
+
+    def stream(b, before, count, state):
         def part(p, state):
-            t = b * parts + p
+            t = before + p
             slot = lax.rem(t, SLOTS)
             copy(slot, b, p).wait()
-
-            def mode(i, state):
-                f0, f1, f2, pot = state
-                k = p * PART + i
-                wr, wi = w[k], w[modes + k]
-                c = ring[slot, i, 0]
-                s = ring[slot, i, 1]
-                pot = pot + (wr * c + wi * s)
-                g = wr * s - wi * c
-                return (
-                    f0 + w[2 * modes + k] * g,
-                    f1 + w[3 * modes + k] * g,
-                    f2 + w[4 * modes + k] * g,
-                    pot,
-                )
-
-            state = lax.fori_loop(0, PART, mode, state, unroll=UNROLL)
-
-            @pl.when(t + SLOTS < blocks * parts)
+            state = run(ring.at[slot], p * PART, state)
+
+            @pl.when(t + SLOTS < n_parts)
             def _():
                 fetch(t + SLOTS)
 
             return state
 
-        state = lax.fori_loop(0, parts, part, (zero,) * 4)
+        state = lax.fori_loop(0, count, part, state)
         for t in range(2):
             for c in range(4):
                 o_ref[2 * b + t, HALF * c : HALF * (c + 1)] = state[c][HALF * t : HALF * (t + 1)]
             o_ref[2 * b + t, 4 * HALF :] = jnp.full((8, 128), energy, jnp.float32)
+
+    stream(blocks - 1, 0, lead, run(keep_ref, modes - KEEP, (zero,) * 4))
+
+    def block(b, carry):
+        stream(b, lead + b * parts, parts, (zero,) * 4)
         return carry
 
-    lax.fori_loop(0, blocks, block, 0)
+    lax.fori_loop(0, blocks - 1, block, 0)
 
 
 def on_device(scaled_coordinate_array, particle_charge_list, reciprocal_triples):
@@ -338,13 +360,15 @@
 
     positive = pltpu.VMEM(((TOP + 1) * ROWS, 128), jnp.float32)
     both = pltpu.VMEM(((2 * TOP + 1) * ROWS, 128), jnp.float32)
-    e, share = pl.pallas_call(
+    e, share, keep, spectrum = pl.pallas_call(
         phases_kernel,
         in_specs=[hbm, hbm, hbm],
-        out_specs=[hbm, vmem],
+        out_specs=[hbm, vmem, vmem, vmem],
         out_shape=[
             jax.ShapeDtypeStruct((blocks, modes, 2, ROWS, 128), jnp.float32),
             pltpu.VMEM((8, 128), jnp.float32),
+            pltpu.VMEM((KEEP, 2, ROWS, 128), jnp.float32),
+            pltpu.VMEM((4 * n_lines, 128), jnp.float32),
         ],
         scratch_shapes=[
             positive,
@@ -373,12 +397,12 @@
 
     terms = pl.pallas_call(
         functools.partial(response_kernel, 50.0 / natoms),
-        in_specs=[vmem, vmem, hbm],
+        in_specs=[vmem, vmem, vmem, hbm],
         out_specs=vmem,
         out_shape=jax.ShapeDtypeStruct((n_kvec, 4 * HALF + 8, 128), jnp.float32),
         scratch_shapes=scalars(jnp.float32) + ring(SLOTS, PART),
         compiler_params=pltpu.CompilerParams(vmem_limit_bytes=32 * MIB),
-    )(got, reciprocal_triples, e)
+    )(got, spectrum, keep, e)
 
     own = lax.all_to_all(terms, "kvec", 0, 0, tiled=True).sum(axis=0)
     energy = own[4 * HALF, 0]

time: 96.4 us -> 94.6 us (0.981)
  Pallas kernels: 48 us -> 47 us
where the time goes in v2:
time: 94.6 us; the launch traced here: 94.3 us
  Pallas kernels  47 us (50%)
  blocking collectives  32.4 us (34%)
  waiting for transfers between devices  6.49 us (7%)
  starting transfers between devices  4.89 us (5%)
  other arithmetic  1.54 us (2%)
  local copies, waits for them, and re-layouts  1.34 us (1%)
    pallas_call x1, Pallas kernels, on_device(): pl.pallas_call(phases_kernel, in_specs=[hbm, hbm, hbm], out_specs=[hbm, v...  26.5 us
    all_to_all x1, blocking collectives, on_device(): lax.all_to_all(share, 'atom', 0, 0, tiled=True, axis_index_groups=cores)  20.5 us
    pallas_call x1, Pallas kernels, on_device(): pl.pallas_call(functools.partial(response_kernel, 50.0 / natoms), in_spec...  20.4 us
    all_to_all x1, blocking collectives, on_device(): own = lax.all_to_all(terms, 'kvec', 0, 0, tiled=True).sum(axis=0)  11.9 us
    all_to_all x1, waiting for transfers between devices, on_device(): summed = lax.all_to_all(copies, 'kvec', 0, 0, tiled=True)  5.33 us
    all_to_all x1, starting transfers between devices, on_device(): summed = lax.all_to_all(copies, 'kvec', 0, 0, tiled=True)  4.8 us
  transfers between devices with their start and end apart: 2, of which 2 were waited for; matrix products, arithmetic and copies ran while one was open for 1% of the time, Pallas kernels for 0%

profile of v2, /device:TPU:2, one launch (start us, length us, event | category | flops | bytes accessed | tf_op | source)
XLA Modules:
  0.0 94.3 jit_solution(17307961889246935681)
XLA Ops:
  0.6 0.0 copy-start
  0.6 26.5 %shard_map.58 = (f32[4,512,2,32,128]{4,3,2,1,0:T(8,128)}, f32[8,128]{1,0:T(8,128)S(1)}, f32[64,2,32,128]{3,2,1,0:T(8,128)S(1)}, f32[16,128]{1,0:T(8,128)S(1)}) custom-call(s32[3,512]{1,0:T(4,128)} %trip_hbm.1, f32[3,16384]{1,0:T(4,128)} %x_hbm.1, f32[128,128]{1,0:T(8,128)} %bitcast.9), custom_call_target="tpu_custom_call" | custom-call | tf_op jit(solution)/shard_map/pallas_call | solution.py:363
  27.2 0.1 collective-permute-start
  27.3 1.2 %collective-permute-done = f32[8,128]{1,0:T(8,128)S(1)} collective-permute-done((f32[8,128]{1,0:T(8,128)S(1)}, f32[8,128]{1,0:T(8,128)S(1)}, u32[]{:S(2)}, u32[]{:S(2)}) %collective-permute-start) | collective-permute-done | bytes 4128 | tf_op jit(solution)/shard_map/ppermute | solution.py:393
  28.4 20.5 %all_to_all.15.got_ref = f32[16,8,128]{2,1,0:T(8,128)S(1)} all-to-all(f32[16,8,128]{2,1,0:T(8,128)S(1)} %broadcast_in_dim.5), channel_id=1, replica_groups={{0,16,32,48,64,80,96,112,128,144,160,176,192,208,224,240},{8,24,40,56,7..., dimensions={0} | all-to-all | bytes 131072 | tf_op jit(solution)/shard_map/all_to_all | solution.py:396
  48.9 20.4 %shard_map.59 = f32[8,72,128]{2,1,0:T(8,128)S(1)} custom-call(f32[16,8,128]{2,1,0:T(8,128)S(1)} %all_to_all.15.got_ref, f32[16,128]{1,0:T(8,128)S(1)} %get-tuple-element.8.modes_ref, f32[64,2,32,128]{3,2,1,0:T(8,128)S(1)} %get-tuple-element.9.keep_ref, f32[4,512,2,32,128]{4,3,2,1,0:T(8,128)} %get-tuple-element.10.e_ref), custom_call_target="tpu_custom_call" | custom-call | tf_op jit(solution)/shard_map/pallas_call | solution.py:398
  69.4 11.9 %all_to_all.16 = f32[8,72,128]{2,1,0:T(8,128)S(1)} all-to-all(f32[8,72,128]{2,1,0:T(8,128)S(1)} %shard_map.59), channel_id=1, replica_groups=mesh['atom'=32,'kvec'=8] {'kvec'}, dimensions={0} | all-to-all | bytes 589824 | tf_op jit(solution)/shard_map/all_to_all | solution.py:407
  81.3 0.7 broadcast_in_dim.6
  82.0 4.8 %all-to-all-start.2 = ((f32[8,64,128]{2,1,0:T(8,128)}), f32[8,64,128]{2,1,0:T(8,128)S(1)}, u32[]{:S(2)}, u32[]{:S(2)}) async-start(f32[8,64,128]{2,1,0:T(8,128)} %broadcast_in_dim.6), calls=%async_computation.2 | async-start | bytes 524288 | tf_op jit(solution)/shard_map/all_to_all | solution.py:410
  86.8 0.5 slice.21
  87.4 5.3 %all-to-all-done.2 = f32[8,64,128]{2,1,0:T(8,128)S(1)} async-done(((f32[8,64,128]{2,1,0:T(8,128)}), f32[8,64,128]{2,1,0:T(8,128)S(1)}, u32[]{:S(2)}, u32[]{:S(2)}) %all-to-all-start.2) | async-done | bytes 262176 | tf_op jit(solution)/shard_map/all_to_all | solution.py:410
  92.7 0.1 reshape.23
  92.8 0.1 slice_multiply_fusion.1
  92.9 0.8 slice_multiply_fusion
  93.7 0.0 copy-done
  93.7 0.6 select_divide_fusion
  (4 shorter events, 0.0 us)
Async XLA Ops:
  0.6 93.0 %copy-start = (f32[16384]{0:T(1024)S(1)}, f32[16384]{0:T(1024)}, u32[]{:S(2)}) copy-start(f32[16384]{0:T(1024)} %param.4) | copy-start | bytes 196612
  27.2 1.3 %collective-permute-start = (f32[8,128]{1,0:T(8,128)S(1)}, f32[8,128]{1,0:T(8,128)S(1)}, u32[]{:S(2)}, u32[]{:S(2)}) collective-permute-start(f32[8,128]{1,0:T(8,128)S(1)} %get-tuple-element.7), channel_id=1, source_target_pairs={{0,8},{8,0},{16,24},{24,16},{32,40},{40,32},{48,56},{56,48},{64,72... | collective-permute-start | bytes 12296 | tf_op jit(solution)/shard_map/ppermute | solution.py:393
  82.0 10.6 %all-to-all-start.2 = ((f32[8,64,128]{2,1,0:T(8,128)}), f32[8,64,128]{2,1,0:T(8,128)S(1)}, u32[]{:S(2)}, u32[]{:S(2)}) async-start(f32[8,64,128]{2,1,0:T(8,128)} %broadcast_in_dim.6), calls=%async_computation.2 | async-start | bytes 524288 | tf_op jit(solution)/shard_map/all_to_all | solution.py:410

commit v3 on v2

--- a/solution.py
+++ b/solution.py
@@ -228,7 +228,7 @@
         @pl.when(jnp.logical_not(faint))
         def _():
             lax.fori_loop(
-                0, groups, lambda g, c: (group(g, None), c)[1], 0, unroll=UNROLL // GROUP
+                0, groups, lambda g, c: (group(g, None), c)[1], 0, unroll=8
             )
 
     lax.fori_loop(0, blocks, block, 0)
@@ -331,6 +331,21 @@
         return carry
 
     lax.fori_loop(0, blocks - 1, block, 0)
+
+
+def finish_kernel(scale, sum_ref, q_ref, forces_ref, potential_ref):
+    chunks = sum_ref.shape[0]
+
+    def chunk(v, carry):
+        for c in range(3):
+            for r in range(HALF):
+                at = pl.ds(pl.multiple_of((v * HALF + r) * 128, 128), 128)
+                forces_ref[c : c + 1, at] = scale * sum_ref[v, HALF * c + r : HALF * c + r + 1]
+        at = pl.ds(pl.multiple_of(v * HALF, HALF), HALF)
+        potential_ref[at] = (400.0 * scale) * sum_ref[v, 3 * HALF :] / nonzero(q_ref[at])
+        return carry
+
+    lax.fori_loop(0, chunks, chunk, 0)
 
 
 def on_device(scaled_coordinate_array, particle_charge_list, reciprocal_triples):
@@ -408,11 +423,17 @@
     energy = own[4 * HALF, 0]
     copies = jnp.broadcast_to(own[None, : 4 * HALF], (n_kvec, 4 * HALF, 128))
     summed = lax.all_to_all(copies, "kvec", 0, 0, tiled=True)
-    summed = summed.reshape(n_kvec, 4, HALF * 128).transpose(1, 0, 2).reshape(4, local_atoms)
-    scale = 1.0 / math.sqrt(natoms)
-    forces = summed[:3] * scale
-    potential = summed[3] * (400.0 * scale) / nonzero(particle_charge_list)
-    return (forces, potential, energy)
+    forces, potential = pl.pallas_call(
+        functools.partial(finish_kernel, 1.0 / math.sqrt(natoms)),
+        in_specs=[vmem, vmem],
+        out_specs=[vmem, vmem],
+        out_shape=[
+            jax.ShapeDtypeStruct((3, local_atoms), jnp.float32),
+            jax.ShapeDtypeStruct((local_atoms // 128, 128), jnp.float32),
+        ],
+        compiler_params=pltpu.CompilerParams(vmem_limit_bytes=8 * MIB),
+    )(summed, q)
+    return (forces, potential.reshape(local_atoms), energy)
 
 
 def solution(mesh):

time: 94.6 us -> 93.3 us (0.986)
  other arithmetic: 1.54 us -> 0.02 us
    pallas_call x0 -> x1, Pallas kernels: none -> 1.01 us  [on_device(): pl.pallas_call(functools.partial(finish_kernel, 1.0 / math.sqrt(natoms)),...]
where the time goes in v3:
time: 93.3 us; the launch traced here: 93.1 us
  Pallas kernels  47.3 us (51%)
  blocking collectives  32.4 us (35%)
  waiting for transfers between devices  6.49 us (7%)
  starting transfers between devices  4.89 us (5%)
  local copies, waits for them, and re-layouts  1.25 us (1%)
    pallas_call x1, Pallas kernels, on_device(): pl.pallas_call(phases_kernel, in_specs=[hbm, hbm, hbm], out_specs=[hbm, v...  25.9 us
    all_to_all x1, blocking collectives, on_device(): lax.all_to_all(share, 'atom', 0, 0, tiled=True, axis_index_groups=cores)  20.5 us
    pallas_call x1, Pallas kernels, on_device(): pl.pallas_call(functools.partial(response_kernel, 50.0 / natoms), in_spec...  20.4 us
    all_to_all x1, blocking collectives, on_device(): own = lax.all_to_all(terms, 'kvec', 0, 0, tiled=True).sum(axis=0)  11.9 us
    all_to_all x1, waiting for transfers between devices, on_device(): summed = lax.all_to_all(copies, 'kvec', 0, 0, tiled=True)  5.33 us
    all_to_all x1, starting transfers between devices, on_device(): summed = lax.all_to_all(copies, 'kvec', 0, 0, tiled=True)  4.8 us
  transfers between devices with their start and end apart: 2, of which 2 were waited for; matrix products, arithmetic and copies ran while one was open for 1% of the time, Pallas kernels for 0%

profile of v3, /device:TPU:2, one launch (start us, length us, event | category | flops | bytes accessed | tf_op | source)
XLA Modules:
  0.0 93.1 jit_solution(12384431897287014168)
XLA Ops:
  0.6 0.0 copy-start
  0.6 25.9 %shard_map.58 = (f32[4,512,2,32,128]{4,3,2,1,0:T(8,128)}, f32[8,128]{1,0:T(8,128)S(1)}, f32[64,2,32,128]{3,2,1,0:T(8,128)S(1)}, f32[16,128]{1,0:T(8,128)S(1)}) custom-call(s32[3,512]{1,0:T(4,128)} %trip_hbm.1, f32[3,16384]{1,0:T(4,128)} %x_hbm.1, f32[128,128]{1,0:T(8,128)} %bitcast.3), custom_call_target="tpu_custom_call" | custom-call | tf_op jit(solution)/shard_map/pallas_call | solution.py:378
  26.6 0.1 collective-permute-start
  26.7 1.2 %collective-permute-done = f32[8,128]{1,0:T(8,128)S(1)} collective-permute-done((f32[8,128]{1,0:T(8,128)S(1)}, f32[8,128]{1,0:T(8,128)S(1)}, u32[]{:S(2)}, u32[]{:S(2)}) %collective-permute-start) | collective-permute-done | bytes 4128 | tf_op jit(solution)/shard_map/ppermute | solution.py:408
  27.8 20.5 %all_to_all.15.got_ref = f32[16,8,128]{2,1,0:T(8,128)S(1)} all-to-all(f32[16,8,128]{2,1,0:T(8,128)S(1)} %broadcast_in_dim.4), channel_id=1, replica_groups={{0,16,32,48,64,80,96,112,128,144,160,176,192,208,224,240},{8,24,40,56,7..., dimensions={0} | all-to-all | bytes 131072 | tf_op jit(solution)/shard_map/all_to_all | solution.py:411
  48.3 20.4 %shard_map.59 = f32[8,72,128]{2,1,0:T(8,128)S(1)} custom-call(f32[16,8,128]{2,1,0:T(8,128)S(1)} %all_to_all.15.got_ref, f32[16,128]{1,0:T(8,128)S(1)} %get-tuple-element.10.modes_ref, f32[64,2,32,128]{3,2,1,0:T(8,128)S(1)} %get-tuple-element.11.keep_ref, f32[4,512,2,32,128]{4,3,2,1,0:T(8,128)} %get-tuple-element.12.e_ref), custom_call_target="tpu_custom_call" | custom-call | tf_op jit(solution)/shard_map/pallas_call | solution.py:413
  68.7 11.9 %all_to_all.16 = f32[8,72,128]{2,1,0:T(8,128)S(1)} all-to-all(f32[8,72,128]{2,1,0:T(8,128)S(1)} %shard_map.59), channel_id=1, replica_groups=mesh['atom'=32,'kvec'=8] {'kvec'}, dimensions={0} | all-to-all | bytes 589824 | tf_op jit(solution)/shard_map/all_to_all | solution.py:422
  80.7 0.7 broadcast_in_dim.5
  81.4 4.8 %all-to-all-start.2 = ((f32[8,64,128]{2,1,0:T(8,128)}), f32[8,64,128]{2,1,0:T(8,128)S(1)}, u32[]{:S(2)}, u32[]{:S(2)}) async-start(f32[8,64,128]{2,1,0:T(8,128)} %broadcast_in_dim.5), calls=%async_computation.2 | async-start | bytes 524288 | tf_op jit(solution)/shard_map/all_to_all | solution.py:425
  86.2 0.5 slice.9
  86.7 5.3 %all-to-all-done.2.sum_ref = f32[8,64,128]{2,1,0:T(8,128)S(1)} async-done(((f32[8,64,128]{2,1,0:T(8,128)}), f32[8,64,128]{2,1,0:T(8,128)S(1)}, u32[]{:S(2)}, u32[]{:S(2)}) %all-to-all-start.2) | async-done | bytes 262176 | tf_op jit(solution)/shard_map/all_to_all | solution.py:425
  92.1 0.0 copy-done
  92.1 1.0 %shard_map.60 = (f32[3,16384]{1,0:T(4,128)}, f32[128,128]{1,0:T(8,128)}) custom-call(f32[8,64,128]{2,1,0:T(8,128)S(1)} %all-to-all-done.2.sum_ref, f32[128,128]{1,0:T(8,128)S(1)} %bitcast.4), custom_call_target="tpu_custom_call" | custom-call | tf_op jit(solution)/shard_map/pallas_call | solution.py:426
  (4 shorter events, 0.0 us)
Async XLA Ops:
  0.6 91.4 %copy-start = (f32[16384]{0:T(1024)S(1)}, f32[16384]{0:T(1024)}, u32[]{:S(2)}) copy-start(f32[16384]{0:T(1024)} %param.4) | copy-start | bytes 196612
  26.6 1.3 %collective-permute-start = (f32[8,128]{1,0:T(8,128)S(1)}, f32[8,128]{1,0:T(8,128)S(1)}, u32[]{:S(2)}, u32[]{:S(2)}) collective-permute-start(f32[8,128]{1,0:T(8,128)S(1)} %get-tuple-element.9), channel_id=1, source_target_pairs={{0,8},{8,0},{16,24},{24,16},{32,40},{40,32},{48,56},{56,48},{64,72... | collective-permute-start | bytes 12296 | tf_op jit(solution)/shard_map/ppermute | solution.py:408
  81.4 10.6 %all-to-all-start.2 = ((f32[8,64,128]{2,1,0:T(8,128)}), f32[8,64,128]{2,1,0:T(8,128)S(1)}, u32[]{:S(2)}, u32[]{:S(2)}) async-start(f32[8,64,128]{2,1,0:T(8,128)} %broadcast_in_dim.5), calls=%async_computation.2 | async-start | bytes 524288 | tf_op jit(solution)/shard_map/all_to_all | solution.py:425

commit v4 on v3

--- a/solution.py
+++ b/solution.py
@@ -333,7 +333,17 @@
     lax.fori_loop(0, blocks - 1, block, 0)
 
 
-def finish_kernel(scale, sum_ref, q_ref, forces_ref, potential_ref):
+def gather_kernel(terms_ref, copies_ref, energy_ref):
+    total = terms_ref[0]
+    for i in range(1, terms_ref.shape[0]):
+        total = total + terms_ref[i]
+    for i in range(copies_ref.shape[0]):
+        copies_ref[i] = total[: 4 * HALF]
+    energy_ref[...] = total[4 * HALF :]
+
+
+def finish_kernel(scale, sum_ref, q_ref, total_ref, forces_ref, potential_ref, energy_ref):
+    energy_ref[0, 0] = jnp.max(total_ref[...])
     chunks = sum_ref.shape[0]
 
     def chunk(v, carry):
@@ -419,21 +429,30 @@
         compiler_params=pltpu.CompilerParams(vmem_limit_bytes=32 * MIB),
     )(got, spectrum, keep, e)
 
-    own = lax.all_to_all(terms, "kvec", 0, 0, tiled=True).sum(axis=0)
-    energy = own[4 * HALF, 0]
-    copies = jnp.broadcast_to(own[None, : 4 * HALF], (n_kvec, 4 * HALF, 128))
+    terms = lax.all_to_all(terms, "kvec", 0, 0, tiled=True)
+    copies, total = pl.pallas_call(
+        gather_kernel,
+        in_specs=[vmem],
+        out_specs=[vmem, vmem],
+        out_shape=[
+            pltpu.VMEM((n_kvec, 4 * HALF, 128), jnp.float32),
+            jax.ShapeDtypeStruct((8, 128), jnp.float32),
+        ],
+        compiler_params=pltpu.CompilerParams(vmem_limit_bytes=8 * MIB),
+    )(terms)
     summed = lax.all_to_all(copies, "kvec", 0, 0, tiled=True)
-    forces, potential = pl.pallas_call(
+    forces, potential, energy = pl.pallas_call(
         functools.partial(finish_kernel, 1.0 / math.sqrt(natoms)),
-        in_specs=[vmem, vmem],
-        out_specs=[vmem, vmem],
+        in_specs=[vmem, vmem, vmem],
+        out_specs=[vmem, vmem, pl.BlockSpec(memory_space=pltpu.SMEM)],
         out_shape=[
             jax.ShapeDtypeStruct((3, local_atoms), jnp.float32),
             jax.ShapeDtypeStruct((local_atoms // 128, 128), jnp.float32),
+            jax.ShapeDtypeStruct((1, 1), jnp.float32),
         ],
         compiler_params=pltpu.CompilerParams(vmem_limit_bytes=8 * MIB),
-    )(summed, q)
-    return (forces, potential.reshape(local_atoms), energy)
+    )(summed, q, total)
+    return (forces, potential.reshape(local_atoms), energy.reshape(()))
 
 
 def solution(mesh):

time: 93.3 us -> 91.7 us (0.983)
  blocking collectives: 32.4 us -> 42.1 us
  waiting for transfers between devices: 6.49 us -> 1.15 us
  starting transfers between devices: 4.89 us -> 0.09 us
  local copies, waits for them, and re-layouts: 1.25 us -> 0.01 us
    all_to_all x1 -> x2, blocking collectives: 11.9 us -> 21.6 us  [the longest x1 11.9 us: on_device(): terms = lax.all_to_all(terms, 'kvec', 0, 0, tiled=True)]
    all_to_all x1 -> x0, waiting for transfers between devices: 5.33 us -> none  [on_device(): summed = lax.all_to_all(copies, 'kvec', 0, 0, tiled=True)]
    all_to_all x1 -> x0, starting transfers between devices: 4.8 us -> none  [on_device(): summed = lax.all_to_all(copies, 'kvec', 0, 0, tiled=True)]
  transfers between devices with their start and end apart: 2 -> 1, of which waited for: 2 -> 1; matrix products, arithmetic and copies ran while one was open for 1% -> 0% of each run, Pallas kernels for 0% -> 0%
where the time goes in v4:
time: 91.7 us; the launch traced here: 91.5 us
  Pallas kernels  47.5 us (52%)
  blocking collectives  42.1 us (46%)
  waiting for transfers between devices  1.15 us (1%)
    pallas_call x1, Pallas kernels, on_device(): pl.pallas_call(phases_kernel, in_specs=[hbm, hbm, hbm], out_specs=[hbm, v...  25.9 us
    all_to_all x1, blocking collectives, on_device(): lax.all_to_all(share, 'atom', 0, 0, tiled=True, axis_index_groups=cores)  20.5 us
    pallas_call x1, Pallas kernels, on_device(): pl.pallas_call(functools.partial(response_kernel, 50.0 / natoms), in_spec...  20.4 us
    all_to_all x1, blocking collectives, on_device(): terms = lax.all_to_all(terms, 'kvec', 0, 0, tiled=True)  11.9 us
    all_to_all x1, blocking collectives, on_device(): summed = lax.all_to_all(copies, 'kvec', 0, 0, tiled=True)  9.7 us
  transfers between devices with their start and end apart: 1, of which 1 were waited for; matrix products, arithmetic and copies ran while one was open for 0% of the time, Pallas kernels for 0%

profile of v4, /device:TPU:2, one launch (start us, length us, event | category | flops | bytes accessed | tf_op | source)
XLA Modules:
  0.0 91.5 jit_solution(13953779870546562577)
XLA Ops:
  0.6 0.0 copy-start
  0.6 25.9 %shard_map.58 = (f32[4,512,2,32,128]{4,3,2,1,0:T(8,128)}, f32[8,128]{1,0:T(8,128)S(1)}, f32[64,2,32,128]{3,2,1,0:T(8,128)S(1)}, f32[16,128]{1,0:T(8,128)S(1)}) custom-call(s32[3,512]{1,0:T(4,128)} %trip_hbm.1, f32[3,16384]{1,0:T(4,128)} %x_hbm.1, f32[128,128]{1,0:T(8,128)} %bitcast.3), custom_call_target="tpu_custom_call" | custom-call | tf_op jit(solution)/shard_map/pallas_call | solution.py:388
  26.6 0.1 collective-permute-start
  26.7 1.2 %collective-permute-done = f32[8,128]{1,0:T(8,128)S(1)} collective-permute-done((f32[8,128]{1,0:T(8,128)S(1)}, f32[8,128]{1,0:T(8,128)S(1)}, u32[]{:S(2)}, u32[]{:S(2)}) %collective-permute-start) | collective-permute-done | bytes 4128 | tf_op jit(solution)/shard_map/ppermute | solution.py:418
  27.8 20.5 %all_to_all.15.got_ref = f32[16,8,128]{2,1,0:T(8,128)S(1)} all-to-all(f32[16,8,128]{2,1,0:T(8,128)S(1)} %broadcast_in_dim.2), channel_id=1, replica_groups={{0,16,32,48,64,80,96,112,128,144,160,176,192,208,224,240},{8,24,40,56,7..., dimensions={0} | all-to-all | bytes 131072 | tf_op jit(solution)/shard_map/all_to_all | solution.py:421
  48.3 20.4 %shard_map.59 = f32[8,72,128]{2,1,0:T(8,128)S(1)} custom-call(f32[16,8,128]{2,1,0:T(8,128)S(1)} %all_to_all.15.got_ref, f32[16,128]{1,0:T(8,128)S(1)} %get-tuple-element.13.modes_ref, f32[64,2,32,128]{3,2,1,0:T(8,128)S(1)} %get-tuple-element.14.keep_ref, f32[4,512,2,32,128]{4,3,2,1,0:T(8,128)} %get-tuple-element.15.e_ref), custom_call_target="tpu_custom_call" | custom-call | tf_op jit(solution)/shard_map/pallas_call | solution.py:423
  68.7 11.9 %all_to_all.16.terms_ref = f32[8,72,128]{2,1,0:T(8,128)S(1)} all-to-all(f32[8,72,128]{2,1,0:T(8,128)S(1)} %shard_map.59), channel_id=1, replica_groups=mesh['atom'=32,'kvec'=8] {'kvec'}, dimensions={0} | all-to-all | bytes 589824 | tf_op jit(solution)/shard_map/all_to_all | solution.py:432
  80.7 9.7 %all_to_all.17.sum_ref = f32[8,64,128]{2,1,0:T(8,128)S(1)} all-to-all(f32[8,64,128]{2,1,0:T(8,128)S(1)} %get-tuple-element.16), channel_id=1, replica_groups=mesh['atom'=32,'kvec'=8] {'kvec'}, dimensions={0} | all-to-all | bytes 524288 | tf_op jit(solution)/shard_map/all_to_all | solution.py:443
  90.4 0.0 copy-done
  90.4 1.1 %shard_map.61 = (f32[3,16384]{1,0:T(4,128)}, f32[128,128]{1,0:T(8,128)}, f32[1,1]{1,0:T(1,128)}) custom-call(f32[8,64,128]{2,1,0:T(8,128)S(1)} %all_to_all.17.sum_ref, f32[128,128]{1,0:T(8,128)S(1)} %bitcast.4, f32[8,128]{1,0:T(8,128)S(1)} %get-tuple-element.17.total_ref), custom_call_target="tpu_custom_call" | custom-call | tf_op jit(solution)/shard_map/pallas_call | solution.py:444
  (3 shorter events, 0.0 us)
Async XLA Ops:
  0.6 89.8 %copy-start = (f32[16384]{0:T(1024)S(1)}, f32[16384]{0:T(1024)}, u32[]{:S(2)}) copy-start(f32[16384]{0:T(1024)} %param.4) | copy-start | bytes 196612
  26.6 1.3 %collective-permute-start = (f32[8,128]{1,0:T(8,128)S(1)}, f32[8,128]{1,0:T(8,128)S(1)}, u32[]{:S(2)}, u32[]{:S(2)}) collective-permute-start(f32[8,128]{1,0:T(8,128)S(1)} %get-tuple-element.12), channel_id=1, source_target_pairs={{0,8},{8,0},{16,24},{24,16},{32,40},{40,32},{48,56},{56,48},{64,72... | collective-permute-start | bytes 12296 | tf_op jit(solution)/shard_map/ppermute | solution.py:418

commit v5 on v4

--- a/solution.py
+++ b/solution.py
@@ -96,6 +96,10 @@
 
 def nonzero(q):
     return jnp.where(jnp.abs(q) < TINY, TINY, q)
+
+
+def unfold(q):
+    return jnp.where(jnp.abs(q) < TINY, q * (1.0 / TINY), 1.0)
 
 
 def lines(v):
@@ -222,7 +226,7 @@
         @pl.when(faint)
         def _():
             q = q_ref[pl.ds(pl.multiple_of(b * ROWS, ROWS), ROWS)]
-            ratio = q / nonzero(q)
+            ratio = unfold(q)
             lax.fori_loop(0, groups, lambda g, c: (group(g, ratio), c)[1], 0)
 
         @pl.when(jnp.logical_not(faint))
@@ -347,10 +351,11 @@
     chunks = sum_ref.shape[0]
 
     def chunk(v, carry):
-        for c in range(3):
-            for r in range(HALF):
-                at = pl.ds(pl.multiple_of((v * HALF + r) * 128, 128), 128)
-                forces_ref[c : c + 1, at] = scale * sum_ref[v, HALF * c + r : HALF * c + r + 1]
+        for r in range(HALF):
+            at = pl.ds(pl.multiple_of((v * HALF + r) * 128, 128), 128)
+            factor = scale * unfold(q_ref[pl.ds(v * HALF + r, 1)])
+            for c in range(3):
+                forces_ref[c : c + 1, at] = factor * sum_ref[v, HALF * c + r : HALF * c + r + 1]
         at = pl.ds(pl.multiple_of(v * HALF, HALF), HALF)
         potential_ref[at] = (400.0 * scale) * sum_ref[v, 3 * HALF :] / nonzero(q_ref[at])
         return carry

time: 91.7 us -> 92.1 us (level)
  no operation moved by 1% of the time
where the time goes in v5:
time: 92.1 us; the launch traced here: 92.2 us
  Pallas kernels  47.5 us (52%)
  blocking collectives  42.8 us (46%)
  waiting for transfers between devices  1.15 us (1%)
    pallas_call x1, Pallas kernels, on_device(): pl.pallas_call(phases_kernel, in_specs=[hbm, hbm, hbm], out_specs=[hbm, v...  25.9 us
    all_to_all x1, blocking collectives, on_device(): lax.all_to_all(share, 'atom', 0, 0, tiled=True, axis_index_groups=cores)  21.1 us
    pallas_call x1, Pallas kernels, on_device(): pl.pallas_call(functools.partial(response_kernel, 50.0 / natoms), in_spec...  20.4 us
    all_to_all x1, blocking collectives, on_device(): terms = lax.all_to_all(terms, 'kvec', 0, 0, tiled=True)  11.9 us
    all_to_all x1, blocking collectives, on_device(): summed = lax.all_to_all(copies, 'kvec', 0, 0, tiled=True)  9.7 us
  transfers between devices with their start and end apart: 1, of which 1 were waited for; matrix products, arithmetic and copies ran while one was open for 0% of the time, Pallas kernels for 0%

profile of v5, /device:TPU:2, one launch (start us, length us, event | category | flops | bytes accessed | tf_op | source)
XLA Modules:
  0.0 92.2 jit_solution(9429685793564886050)
XLA Ops:
  0.6 0.0 copy-start
  0.6 25.9 %shard_map.58 = (f32[4,512,2,32,128]{4,3,2,1,0:T(8,128)}, f32[8,128]{1,0:T(8,128)S(1)}, f32[64,2,32,128]{3,2,1,0:T(8,128)S(1)}, f32[16,128]{1,0:T(8,128)S(1)}) custom-call(s32[3,512]{1,0:T(4,128)} %trip_hbm.1, f32[3,16384]{1,0:T(4,128)} %x_hbm.1, f32[128,128]{1,0:T(8,128)} %bitcast.3), custom_call_target="tpu_custom_call" | custom-call | tf_op jit(solution)/shard_map/pallas_call | solution.py:393
  26.6 0.1 collective-permute-start
  26.7 1.2 %collective-permute-done = f32[8,128]{1,0:T(8,128)S(1)} collective-permute-done((f32[8,128]{1,0:T(8,128)S(1)}, f32[8,128]{1,0:T(8,128)S(1)}, u32[]{:S(2)}, u32[]{:S(2)}) %collective-permute-start) | collective-permute-done | bytes 4128 | tf_op jit(solution)/shard_map/ppermute | solution.py:423
  27.8 21.1 %all_to_all.15.got_ref = f32[16,8,128]{2,1,0:T(8,128)S(1)} all-to-all(f32[16,8,128]{2,1,0:T(8,128)S(1)} %broadcast_in_dim.2), channel_id=1, replica_groups={{0,16,32,48,64,80,96,112,128,144,160,176,192,208,224,240},{8,24,40,56,7..., dimensions={0} | all-to-all | bytes 131072 | tf_op jit(solution)/shard_map/all_to_all | solution.py:426
  49.0 20.4 %shard_map.59 = f32[8,72,128]{2,1,0:T(8,128)S(1)} custom-call(f32[16,8,128]{2,1,0:T(8,128)S(1)} %all_to_all.15.got_ref, f32[16,128]{1,0:T(8,128)S(1)} %get-tuple-element.13.modes_ref, f32[64,2,32,128]{3,2,1,0:T(8,128)S(1)} %get-tuple-element.14.keep_ref, f32[4,512,2,32,128]{4,3,2,1,0:T(8,128)} %get-tuple-element.15.e_ref), custom_call_target="tpu_custom_call" | custom-call | tf_op jit(solution)/shard_map/pallas_call | solution.py:428
  69.4 11.9 %all_to_all.16.terms_ref = f32[8,72,128]{2,1,0:T(8,128)S(1)} all-to-all(f32[8,72,128]{2,1,0:T(8,128)S(1)} %shard_map.59), channel_id=1, replica_groups=mesh['atom'=32,'kvec'=8] {'kvec'}, dimensions={0} | all-to-all | bytes 589824 | tf_op jit(solution)/shard_map/all_to_all | solution.py:437
  81.3 9.7 %all_to_all.17.sum_ref = f32[8,64,128]{2,1,0:T(8,128)S(1)} all-to-all(f32[8,64,128]{2,1,0:T(8,128)S(1)} %get-tuple-element.16), channel_id=1, replica_groups=mesh['atom'=32,'kvec'=8] {'kvec'}, dimensions={0} | all-to-all | bytes 524288 | tf_op jit(solution)/shard_map/all_to_all | solution.py:448
  91.0 0.0 copy-done
  91.0 1.2 %shard_map.61 = (f32[3,16384]{1,0:T(4,128)}, f32[128,128]{1,0:T(8,128)}, f32[1,1]{1,0:T(1,128)}) custom-call(f32[8,64,128]{2,1,0:T(8,128)S(1)} %all_to_all.17.sum_ref, f32[128,128]{1,0:T(8,128)S(1)} %bitcast.4, f32[8,128]{1,0:T(8,128)S(1)} %get-tuple-element.17.total_ref), custom_call_target="tpu_custom_call" | custom-call | tf_op jit(solution)/shard_map/pallas_call | solution.py:449
  (3 shorter events, 0.0 us)
Async XLA Ops:
  0.6 90.4 %copy-start = (f32[16384]{0:T(1024)S(1)}, f32[16384]{0:T(1024)}, u32[]{:S(2)}) copy-start(f32[16384]{0:T(1024)} %param.4) | copy-start | bytes 196612
  26.6 1.3 %collective-permute-start = (f32[8,128]{1,0:T(8,128)S(1)}, f32[8,128]{1,0:T(8,128)S(1)}, u32[]{:S(2)}, u32[]{:S(2)}) collective-permute-start(f32[8,128]{1,0:T(8,128)S(1)} %get-tuple-element.12), channel_id=1, source_target_pairs={{0,8},{8,0},{16,24},{24,16},{32,40},{40,32},{48,56},{56,48},{64,72... | collective-permute-start | bytes 12296 | tf_op jit(solution)/shard_map/ppermute | solution.py:423

commit v6 on v5

--- a/solution.py
+++ b/solution.py
@@ -109,7 +109,7 @@
 def to_scalars(stage, scalars, sems):
     return [
         pltpu.make_async_copy(stage.at[i], scalars.at[pl.ds(128 * i, 128)], sems.at[i])
-        for i in range(stage.shape[0])
+        for i in range(sems.shape[0])
     ]
 
 
@@ -284,7 +284,7 @@
     energy = scale * jnp.sum(damping * (cosine * cosine + sine * sine))
     stage[:n_lines] = damping * cosine
     stage[n_lines : 2 * n_lines] = damping * sine
-    stage[2 * n_lines :] = modes_ref[n_lines:]
+    stage[2 * n_lines : 5 * n_lines] = modes_ref[n_lines:]
     for move in to_scalars(stage, w, w_sem):
         move.start()
     for move in to_scalars(stage, w, w_sem):
@@ -383,7 +383,7 @@
 
     def scalars(dtype):
         return [
-            pltpu.VMEM((KINDS * n_lines, 128), dtype),
+            pltpu.VMEM((pl.cdiv(KINDS * n_lines, 8) * 8, 128), dtype),
             pltpu.SMEM((KINDS * modes,), dtype),
             pltpu.SemaphoreType.DMA((KINDS * n_lines,)),
         ]
@@ -407,8 +407,8 @@
             both,
             positive,
             both,
-            pltpu.VMEM((modes * 8, 128), jnp.float32),
-            pltpu.VMEM((modes * 8, 128), jnp.float32),
+            pltpu.VMEM((modes * 8 + 8, 128), jnp.float32),
+            pltpu.VMEM((modes * 8 + 8, 128), jnp.float32),
             pltpu.VMEM((3, modes), jnp.int32),
             pltpu.VMEM((3, local_atoms), jnp.float32),
             pltpu.VMEM((local_atoms // 128, 128), jnp.float32),

time: 92.1 us -> 92.2 us (level)
  no operation moved by 1% of the time
where the time goes in v6:
time: 92.2 us; the launch traced here: 91.7 us
  Pallas kernels  47.6 us (52%)
  blocking collectives  42.1 us (46%)
  waiting for transfers between devices  1.15 us (1%)
    pallas_call x1, Pallas kernels, on_device(): pl.pallas_call(phases_kernel, in_specs=[hbm, hbm, hbm], out_specs=[hbm, v...  26 us
    all_to_all x1, blocking collectives, on_device(): lax.all_to_all(share, 'atom', 0, 0, tiled=True, axis_index_groups=cores)  20.5 us
    pallas_call x1, Pallas kernels, on_device(): pl.pallas_call(functools.partial(response_kernel, 50.0 / natoms), in_spec...  20.4 us
    all_to_all x1, blocking collectives, on_device(): terms = lax.all_to_all(terms, 'kvec', 0, 0, tiled=True)  11.9 us
    all_to_all x1, blocking collectives, on_device(): summed = lax.all_to_all(copies, 'kvec', 0, 0, tiled=True)  9.7 us
  transfers between devices with their start and end apart: 1, of which 1 were waited for; matrix products, arithmetic and copies ran while one was open for 0% of the time, Pallas kernels for 0%

profile of v6, /device:TPU:2, one launch (start us, length us, event | category | flops | bytes accessed | tf_op | source)
XLA Modules:
  0.0 91.7 jit_solution(5019082580799745036)
XLA Ops:
  0.6 0.0 copy-start
  0.6 26.0 %shard_map.58 = (f32[4,512,2,32,128]{4,3,2,1,0:T(8,128)}, f32[8,128]{1,0:T(8,128)S(1)}, f32[64,2,32,128]{3,2,1,0:T(8,128)S(1)}, f32[16,128]{1,0:T(8,128)S(1)}) custom-call(s32[3,512]{1,0:T(4,128)} %trip_hbm.1, f32[3,16384]{1,0:T(4,128)} %x_hbm.1, f32[128,128]{1,0:T(8,128)} %bitcast.3), custom_call_target="tpu_custom_call" | custom-call | tf_op jit(solution)/shard_map/pallas_call | solution.py:393
  26.7 0.1 collective-permute-start
  26.8 1.2 %collective-permute-done = f32[8,128]{1,0:T(8,128)S(1)} collective-permute-done((f32[8,128]{1,0:T(8,128)S(1)}, f32[8,128]{1,0:T(8,128)S(1)}, u32[]{:S(2)}, u32[]{:S(2)}) %collective-permute-start) | collective-permute-done | bytes 4128 | tf_op jit(solution)/shard_map/ppermute | solution.py:423
  27.9 20.5 %all_to_all.15.got_ref = f32[16,8,128]{2,1,0:T(8,128)S(1)} all-to-all(f32[16,8,128]{2,1,0:T(8,128)S(1)} %broadcast_in_dim.2), channel_id=1, replica_groups={{0,16,32,48,64,80,96,112,128,144,160,176,192,208,224,240},{8,24,40,56,7..., dimensions={0} | all-to-all | bytes 131072 | tf_op jit(solution)/shard_map/all_to_all | solution.py:426
  48.4 20.4 %shard_map.59 = f32[8,72,128]{2,1,0:T(8,128)S(1)} custom-call(f32[16,8,128]{2,1,0:T(8,128)S(1)} %all_to_all.15.got_ref, f32[16,128]{1,0:T(8,128)S(1)} %get-tuple-element.13.modes_ref, f32[64,2,32,128]{3,2,1,0:T(8,128)S(1)} %get-tuple-element.14.keep_ref, f32[4,512,2,32,128]{4,3,2,1,0:T(8,128)} %get-tuple-element.15.e_ref), custom_call_target="tpu_custom_call" | custom-call | tf_op jit(solution)/shard_map/pallas_call | solution.py:428
  68.8 11.9 %all_to_all.16.terms_ref = f32[8,72,128]{2,1,0:T(8,128)S(1)} all-to-all(f32[8,72,128]{2,1,0:T(8,128)S(1)} %shard_map.59), channel_id=1, replica_groups=mesh['atom'=32,'kvec'=8] {'kvec'}, dimensions={0} | all-to-all | bytes 589824 | tf_op jit(solution)/shard_map/all_to_all | solution.py:437
  80.8 9.7 %all_to_all.17.sum_ref = f32[8,64,128]{2,1,0:T(8,128)S(1)} all-to-all(f32[8,64,128]{2,1,0:T(8,128)S(1)} %get-tuple-element.16), channel_id=1, replica_groups=mesh['atom'=32,'kvec'=8] {'kvec'}, dimensions={0} | all-to-all | bytes 524288 | tf_op jit(solution)/shard_map/all_to_all | solution.py:448
  90.5 0.0 copy-done
  90.5 1.2 %shard_map.61 = (f32[3,16384]{1,0:T(4,128)}, f32[128,128]{1,0:T(8,128)}, f32[1,1]{1,0:T(1,128)}) custom-call(f32[8,64,128]{2,1,0:T(8,128)S(1)} %all_to_all.17.sum_ref, f32[128,128]{1,0:T(8,128)S(1)} %bitcast.4, f32[8,128]{1,0:T(8,128)S(1)} %get-tuple-element.17.total_ref), custom_call_target="tpu_custom_call" | custom-call | tf_op jit(solution)/shard_map/pallas_call | solution.py:449
  (3 shorter events, 0.0 us)
Async XLA Ops:
  0.6 89.8 %copy-start = (f32[16384]{0:T(1024)S(1)}, f32[16384]{0:T(1024)}, u32[]{:S(2)}) copy-start(f32[16384]{0:T(1024)} %param.4) | copy-start | bytes 196612
  26.7 1.3 %collective-permute-start = (f32[8,128]{1,0:T(8,128)S(1)}, f32[8,128]{1,0:T(8,128)S(1)}, u32[]{:S(2)}, u32[]{:S(2)}) collective-permute-start(f32[8,128]{1,0:T(8,128)S(1)} %get-tuple-element.12), channel_id=1, source_target_pairs={{0,8},{8,0},{16,24},{24,16},{32,40},{40,32},{48,56},{56,48},{64,72... | collective-permute-start | bytes 12296 | tf_op jit(solution)/shard_map/ppermute | solution.py:423
